TPU v7x, 32 devices: a whole 2x2x4 slice. The times are simulated.
32 devices in a mesh: heads: 2 (over x), seq: 16 (over z, y, core).
Axes of the slice: x: 2, y: 2, z: 4, core: 2. Of those that a mesh axis runs over, the one named last changes fastest.
Arguments:
- query_nope: bfloat16 [1, 4, 128, 128], P(None, None, 'heads'), may hold values from -6 to 6
- query_rope: bfloat16 [1, 4, 128, 64], P(None, None, 'heads'), may hold values from -8 to 8
- latent_cache: bfloat16 [1, 8192, 512], P(None, 'seq'), may hold values from -6 to 6
- rope_keys: bfloat16 [1, 64, 8192], P(None, None, 'seq'), may hold values from -8 to 8
- lengths: int32 [1], replicated, may hold values from 2 to 8189, as said below
- key_quant: bfloat16 [128, 512, 128], P('heads', 'seq'), may hold values from -127 to 127, as said below
- key_scale: float32 [128, 4], P('heads'), may hold values from 0.0006 to 0.0024
- value_quant: bfloat16 [128, 512, 128], P('heads', 'seq'), may hold values from -127 to 127, as said below
- value_scale: float32 [128, 4], P('heads'), may hold values from 0.0003 to 0.0012
- out_weight: bfloat16 [16384, 7168], P('heads', 'seq'), may hold values from -0.375 to 0.375
Outputs:
- attn_out: bfloat16 [1, 4, 7168], P(None, None, 'seq')
Inputs may be any that keep to these rules, and one draw needn't show every extreme that they name: `key_quant`: whole numbers. `value_quant`: whole numbers. `lengths`: one sequence has the largest allowed length, so that its last draft token sees all 8192 positions.
All inputs are finite; a program needn't handle non-finite values.
Results may differ from a plain program's by a relative error of at most 0.019.
Values may be sent and summed in bfloat16 or wider, within the bound.
A program may use at most 64 MiB of HBM per device.

v0:
```python
import jax
import jax.numpy as jnp
from jax import lax
from jax.sharding import PartitionSpec as P

QB = 128
neg_large = -1e30


def expand_scales(block_scale, offset, count):
    row_ids = (offset + jnp.arange(count, dtype=jnp.int32)) // QB
    onehot = (
        row_ids[:, None] == jnp.arange(block_scale.shape[1], dtype=jnp.int32)[None, :]
    ).astype(block_scale.dtype)
    return jnp.sum(block_scale[:, None, :] * onehot[None, :, :], axis=2)


def dequantize(quantized, block_scale, offset):
    factors = expand_scales(block_scale, offset, quantized.shape[1])
    return (quantized.astype(jnp.float32) * factors[:, :, None]).astype(jnp.bfloat16)


def per_device(
    query_nope,
    query_rope,
    latent_cache,
    rope_keys,
    lengths,
    key_quant,
    key_scale,
    value_quant,
    value_scale,
    out_weight,
):
    seq_index = lax.axis_index("seq")
    latent_cols = key_quant.shape[1]
    offset = seq_index * latent_cols
    factor = (query_nope.shape[-1] + query_rope.shape[-1]) ** (-0.5)
    key_weight = dequantize(key_quant, key_scale, offset)
    piece_lat = jnp.einsum(
        "btkn,kcn->btkc", query_nope, key_weight, preferred_element_type=jnp.float32
    ).astype(jnp.bfloat16)
    query_latent = lax.all_gather(piece_lat, "seq", axis=3, tiled=True)
    positions = latent_cache.shape[1]
    scores = jnp.einsum(
        "btkc,bsc->btks", query_latent, latent_cache, preferred_element_type=jnp.float32
    )
    scores = (
        scores
        + jnp.einsum("btkr,brs->btks", query_rope, rope_keys, preferred_element_type=jnp.float32)
    ) * factor
    position = seq_index * positions + jnp.arange(positions, dtype=jnp.int32)
    horizon = lengths[:, None] + jnp.arange(query_nope.shape[1], dtype=jnp.int32)[None, :]
    visible = (position[None, None, :] < horizon[:, :, None])[:, :, None, :]
    block_max = jnp.max(jnp.where(visible, scores, neg_large), axis=3)
    probs = jnp.where(visible, jnp.exp(scores - block_max[..., None]), 0.0)
    block_sum = jnp.sum(probs, axis=3)
    probs_bf = probs.astype(jnp.bfloat16)
    block_out = jnp.einsum(
        "btks,bsc->btkc", probs_bf, latent_cache, preferred_element_type=jnp.float32
    )
    top = lax.pmax(block_max, "seq")
    rescale = jnp.exp(block_max - top)
    totals = lax.psum(block_sum * rescale, "seq")
    shrink = jnp.exp(block_max - top)
    merged_slice = lax.psum_scatter(
        block_out * shrink[..., None], "seq", scatter_dimension=3, tiled=True
    )
    latent_slice = (merged_slice / totals[..., None]).astype(jnp.bfloat16)
    value_weight = dequantize(value_quant, value_scale, offset)
    partial_heads = jnp.einsum(
        "btkc,kcv->btkv", latent_slice, value_weight, preferred_element_type=jnp.float32
    )
    flat_terms = partial_heads.reshape(-1)
    share_sum = lax.psum_scatter(flat_terms, "seq", scatter_dimension=0, tiled=True).astype(
        jnp.bfloat16
    )
    head_output = lax.all_gather(share_sum, "seq", axis=0, tiled=True).reshape(partial_heads.shape)
    batch, drafts, heads_here, value_width = head_output.shape
    projected = jnp.dot(
        head_output.reshape(batch * drafts, heads_here * value_width),
        out_weight,
        preferred_element_type=jnp.float32,
    )
    summed = lax.psum(projected, "heads")
    return summed.astype(jnp.bfloat16).reshape(batch, drafts, out_weight.shape[1])


def solution(mesh):
    in_specs = (
        P(None, None, "heads", None),
        P(None, None, "heads", None),
        P(None, "seq", None),
        P(None, None, "seq"),
        P(),
        P("heads", "seq", None),
        P("heads", None),
        P("heads", "seq", None),
        P("heads", None),
        P("heads", "seq"),
    )
    out_specs = P(None, None, "seq")
    return jax.shard_map(
        per_device, mesh=mesh, in_specs=in_specs, out_specs=out_specs, check_vma=False
    )
```

profile of v0, /device:TPU:0, one launch (start us, length us, event | category | flops | bytes accessed | tf_op | source)
XLA Modules:
  0.0 255.0 jit_solution(11461911653005468374)
XLA Ops:
  6.5 0.0 copy-start
  6.5 0.0 copy-start.2
  6.5 0.0 copy-start.1
  6.5 0.0 all-reduce.5.cloned.1.call-start
  7.3 0.8 multiply_reduce_fusion.1
  8.1 0.1 copy.31
  8.2 1.5 fusion.2
  9.7 0.1 copy.33
  9.8 24.6 %all_gather.6 = bf16[1,4,64,512]{2,1,0,3:T(4,128)(2,1)S(1)} all-gather(bf16[1,4,64,32]{2,1,0,3:T(4,128)(2,1)S(1)} %copy.33), channel_id=1, replica_groups=mesh['heads'=2,'seq'=16] {'seq'}, dimensions={3}, use_global_device_ids=true | all-gather | bytes 278528 | tf_op jit(solution)/shard_map/all_gather | solution.py:43
  34.4 0.3 copy.34
  34.7 0.1 broadcast_compare_fusion
  34.8 0.0 copy-done
  34.8 0.3 fusion.4
  35.2 1.2 select_reduce_fusion
  36.3 29.8 %pmax.7 = f32[1,4,64]{2,1,0:T(4,128)S(1)} all-reduce(f32[1,4,64]{2,1,0:T(4,128)S(1)} %bitcast.55), channel_id=1, replica_groups=mesh['heads'=2,'seq'=16] {'seq'}, use_global_device_ids=true, to_apply=%region_3.4 | all-reduce | flops 256 | bytes 2048 | tf_op jit(solution)/shard_map/pmax | solution.py:62
  66.2 0.2 fusion.8
  66.4 0.4 fusion.1
  66.8 1.4 copy.35
  68.1 0.0 all-reduce.5.cloned.1.call-update
  68.2 0.0 copy-done.2
  68.2 0.6 dynamic-slice
  69.4 0.1 copy.30
  70.2 29.5 %psum.14 = f32[4,64]{1,0:T(4,128)S(1)} all-reduce(f32[4,64]{1,0:T(4,128)S(1)} %get-tuple-element.8), channel_id=1, replica_groups=mesh['heads'=2,'seq'=16] {'seq'}, use_global_device_ids=true, to_apply=%region_6.7 | all-reduce | flops 256 | bytes 2048 | tf_op jit(solution)/shard_map/psum | solution.py:64
  99.7 59.7 %all-reduce.5.cloned.1.call-done = f32[1,4,64,512]{2,1,0,3:T(4,128)} async-done(((f32[1,4,64,512]{2,1,0,3:T(4,128)}), f32[1,4,64,512]{2,1,0,3:T(4,128)}) %all-reduce.5.cloned.1.call-update) | async-done | bytes 524304
  159.4 0.9 fusion.19
  160.2 0.1 copy.36
  160.4 0.0 copy-done.1
  160.4 0.4 convolution_bitcast_fusion
  160.8 59.3 %all-reduce.6 = bf16[32768]{0:T(1024)(128)(2,1)S(1)} all-reduce(f32[32768]{0:T(1024)S(1)} %bitcast.54), channel_id=3, replica_groups=mesh['heads'=2,'seq'=16] {'seq'}, use_global_device_ids=true, to_apply=%region_7.8.clone | all-reduce | flops 32768 | bytes 196608
  220.1 17.3 %all_gather.7 = bf16[32768]{0:T(1024)(128)(2,1)S(1)} all-gather(bf16[2048]{0:T(1024)(128)(2,1)S(1)} %dynamic-slice.10), channel_id=1, replica_groups=mesh['heads'=2,'seq'=16] {'seq'}, dimensions={0}, use_global_device_ids=true | all-gather | bytes 69632 | tf_op jit(solution)/shard_map/all_gather | solution.py:78
  237.5 5.1 %fusion.24 = f32[4,448]{1,0:T(4,128)S(1)} fusion(bf16[4,8192]{1,0:T(4,128)(2,1)S(1)} %reshape_reshape.3, bf16[8192,448]{0,1:T(8,128)(2,1)} %param.19), kind=kOutput, calls=%fused_computation.46 | convolution fusion | flops 29360128 | bytes 7412736 | tf_op jit(solution)/shard_map/dot_general | solution.py:80
  242.5 5.6 %psum.15 = bf16[4,448]{1,0:T(4,128)(2,1)} all-reduce(f32[4,448]{1,0:T(4,128)S(1)} %fusion.24), channel_id=1, replica_groups=mesh['heads'=2,'seq'=16] {'heads'}, use_global_device_ids=true, to_apply=%region_8.9 | all-reduce | flops 1792 | bytes 10752 | tf_op jit(solution)/shard_map/psum | solution.py:85
  (8 shorter events, 0.1 us)
Async XLA Ops:
  6.5 28.3 %copy-start = (bf16[1,512,512]{2,1,0:T(8,128)(2,1)S(1)}, bf16[1,512,512]{2,1,0:T(8,128)(2,1)}, u32[]{:S(2)}) copy-start(bf16[1,512,512]{2,1,0:T(8,128)(2,1)} %param.12) | copy-start | bytes 1572868
  6.5 61.6 %copy-start.2 = (u32[32]{0:T(128)S(1)}, u32[32]{0:T(128)}, u32[]{:S(2)}) copy-start(u32[32]{0:T(128)} %constant.36) | copy-start | bytes 388
  6.5 153.8 %copy-start.1 = (bf16[64,32,128]{2,1,0:T(8,128)(2,1)S(1)}, bf16[64,32,128]{2,1,0:T(8,128)(2,1)}, u32[]{:S(2)}) copy-start(bf16[64,32,128]{2,1,0:T(8,128)(2,1)} %param.17) | copy-start | bytes 1572868
  6.5 152.8 %all-reduce.5.cloned.1.call-start = ((), (), s32[]{:S(2)}) async-start(), calls=%async_computation | async-start | bytes 2097152
Sparse Core Ops, SparseCore 0:
  68.3 91.0 all-reduce.4
where the time goes:
time: 255 us
  blocking collectives  166 us (65%)
  waiting for transfers between devices  59.7 us (23%)
  between operations  15.6 us (6%)
  matrix products  8.86 us (3%)
  local copies, waits for them, and re-layouts  2.7 us (1%)
    unnamed x2, waiting for transfers between devices  59.7 us
    unnamed x1, blocking collectives  59.3 us
    pmax x1, blocking collectives, per_device(): top = lax.pmax(block_max, 'seq')  29.8 us
    psum x1, blocking collectives, per_device(): totals = lax.psum(block_sum * rescale, 'seq')  29.5 us
    all_gather x1, blocking collectives, per_device(): query_latent = lax.all_gather(piece_lat, 'seq', axis=3, tiled=True)  24.6 us
    all_gather x1, blocking collectives, per_device(): lax.all_gather(share_sum, 'seq', axis=0, tiled=True)  17.3 us
    psum x1, blocking collectives, per_device(): summed = lax.psum(projected, 'heads')  5.57 us
  transfers between devices with their start and end apart: 1, of which 1 were waited for; matrix products, arithmetic and copies ran while one was open for 0% of the time, Pallas kernels for 0%

commit v1 on v0

--- a/solution.py
+++ b/solution.py
@@ -40,11 +40,28 @@
     piece_lat = jnp.einsum(
         "btkn,kcn->btkc", query_nope, key_weight, preferred_element_type=jnp.float32
     ).astype(jnp.bfloat16)
-    query_latent = lax.all_gather(piece_lat, "seq", axis=3, tiled=True)
     positions = latent_cache.shape[1]
-    scores = jnp.einsum(
-        "btkc,bsc->btks", query_latent, latent_cache, preferred_element_type=jnp.float32
+    peers, place = (lax.axis_size("seq"), lax.axis_index("seq"))
+    downward = [(i, (i - 1) % peers) for i in range(peers)]
+    rows = piece_lat.shape[3]
+    held = piece_lat
+    total = jnp.einsum(
+        "btkc,bsc->btks",
+        held,
+        lax.dynamic_slice_in_dim(latent_cache, place * rows, held.shape[3], axis=2),
+        preferred_element_type=jnp.float32,
     )
+    for step in range(1, peers):
+        held = lax.ppermute(held, "seq", downward)
+        total = total + jnp.einsum(
+            "btkc,bsc->btks",
+            held,
+            lax.dynamic_slice_in_dim(
+                latent_cache, (place + step) % peers * rows, held.shape[3], axis=2
+            ),
+            preferred_element_type=jnp.float32,
+        )
+    scores = total
     scores = (
         scores
         + jnp.einsum("btkr,brs->btks", query_rope, rope_keys, preferred_element_type=jnp.float32)

time: 255 us -> 330 us (1.29)
  starting transfers between devices: 0.01 us -> 67.8 us
  waiting for transfers between devices: 59.7 us -> 81.9 us
  blocking collectives: 166 us -> 146 us
  matrix products: 8.86 us -> 13.5 us
    ppermute x0 -> x15, starting transfers between devices: none -> 67.8 us  [per_device(): held = lax.ppermute(held, 'seq', downward)]
    all_gather x1 -> x0, blocking collectives: 24.6 us -> none  [per_device(): query_latent = lax.all_gather(piece_lat, 'seq', axis=3, tiled=True)]
    ppermute x0 -> x15, waiting for transfers between devices: none -> 22.3 us  [per_device(): held = lax.ppermute(held, 'seq', downward)]
    dot_general x1 -> x16, matrix products: 0.33 us -> 5.06 us  [per_device(): jnp.einsum('btkc,bsc->btks', held, lax.dynamic_slice_in_dim(latent_cache,...]
    pmax x1, blocking collectives: 29.8 us -> 34 us  [per_device(): top = lax.pmax(block_max, 'seq')]
  transfers between devices with their start and end apart: 1 -> 16, of which waited for: 1 -> 15; matrix products, arithmetic and copies ran while one was open for 0% -> 2% of each run, Pallas kernels for 0% -> 0%
where the time goes in v1:
time: 330 us; the launch traced here: 329 us
  blocking collectives  146 us (44%)
  waiting for transfers between devices  81.9 us (25%)
  starting transfers between devices  67.8 us (21%)
  between operations  15.7 us (5%)
  matrix products  13.5 us (4%)
    ppermute x15, starting transfers between devices, per_device(): held = lax.ppermute(held, 'seq', downward)  67.8 us
    unnamed x2, waiting for transfers between devices  59.6 us
    unnamed x1, blocking collectives  59.3 us
    pmax x1, blocking collectives, per_device(): top = lax.pmax(block_max, 'seq')  34 us
    psum x1, blocking collectives, per_device(): totals = lax.psum(block_sum * rescale, 'seq')  29.8 us
    ppermute x15, waiting for transfers between devices, per_device(): held = lax.ppermute(held, 'seq', downward)  22.3 us
    all_gather x1, blocking collectives, per_device(): lax.all_gather(share_sum, 'seq', axis=0, tiled=True)  17.3 us
  transfers between devices with their start and end apart: 16, of which 15 were waited for; matrix products, arithmetic and copies ran while one was open for 2% of the time, Pallas kernels for 0%

profile of v1, /device:TPU:0, one launch (start us, length us, event | category | flops | bytes accessed | tf_op | source)
XLA Modules:
  0.0 329.2 jit_solution(9395806502377732683)
XLA Ops:
  6.6 0.8 multiply_reduce_fusion.1
  7.4 0.1 copy.123
  7.5 1.5 convolution_convert_fusion
  9.0 5.5 %collective-permute-start = (bf16[1,4,64,32]{3,1,2,0:T(4,128)(2,1)S(1)}, bf16[1,4,64,32]{3,1,2,0:T(4,128)(2,1)S(1)}, u32[]{:S(2)}, u32[]{:S(2)}) collective-permute-start(bf16[1,4,64,32]{3,1,2,0:T(4,128)(2,1)S(1)} %bitcast.145), channel_id=1, source_target_pairs={{0,15},{1,0},{2,1},{3,2},{4,3},{5,4},{6,5},{7,6},{8,7},{9,8},{10,9... | collective-permute-start | bytes 49160 | tf_op jit(solution)/shard_map/ppermute | solution.py:55
  15.2 1.1 fusion.45
  16.3 0.3 fusion.27
  16.8 4.1 %collective-permute-start.1 = (bf16[1,4,64,32]{3,1,2,0:T(4,128)(2,1)S(1)}, bf16[1,4,64,32]{3,1,2,0:T(4,128)(2,1)S(1)}, u32[]{:S(2)}, u32[]{:S(2)}) collective-permute-start(bf16[1,4,64,32]{3,1,2,0:T(4,128)(2,1)S(1)} %collective-permute-done), channel_id=1, source_target_pairs={{0,15},{1,0},{2,1},{3,2},{4,3},{5,4},{6,5},{7,6},{8,7},{9,8},{10,9... | collective-permute-start | bytes 49160 | tf_op jit(solution)/shard_map/ppermute | solution.py:55
  20.9 0.3 convolution_add_fusion.14
  21.2 1.6 collective-permute-done.1
  22.8 4.5 %collective-permute-start.2 = (bf16[1,4,64,32]{3,1,2,0:T(4,128)(2,1)S(1)}, bf16[1,4,64,32]{3,1,2,0:T(4,128)(2,1)S(1)}, u32[]{:S(2)}, u32[]{:S(2)}) collective-permute-start(bf16[1,4,64,32]{3,1,2,0:T(4,128)(2,1)S(1)} %collective-permute-done.1), channel_id=1, source_target_pairs={{0,15},{1,0},{2,1},{3,2},{4,3},{5,4},{6,5},{7,6},{8,7},{9,8},{10,9... | collective-permute-start | bytes 49160 | tf_op jit(solution)/shard_map/ppermute | solution.py:55
  27.3 0.3 convolution_add_fusion.13
  27.6 1.6 collective-permute-done.2
  29.2 4.5 %collective-permute-start.3 = (bf16[1,4,64,32]{3,1,2,0:T(4,128)(2,1)S(1)}, bf16[1,4,64,32]{3,1,2,0:T(4,128)(2,1)S(1)}, u32[]{:S(2)}, u32[]{:S(2)}) collective-permute-start(bf16[1,4,64,32]{3,1,2,0:T(4,128)(2,1)S(1)} %collective-permute-done.2), channel_id=1, source_target_pairs={{0,15},{1,0},{2,1},{3,2},{4,3},{5,4},{6,5},{7,6},{8,7},{9,8},{10,9... | collective-permute-start | bytes 49160 | tf_op jit(solution)/shard_map/ppermute | solution.py:55
  33.7 0.3 convolution_add_fusion.12
  34.0 1.6 collective-permute-done.3
  35.6 4.5 %collective-permute-start.4 = (bf16[1,4,64,32]{3,1,2,0:T(4,128)(2,1)S(1)}, bf16[1,4,64,32]{3,1,2,0:T(4,128)(2,1)S(1)}, u32[]{:S(2)}, u32[]{:S(2)}) collective-permute-start(bf16[1,4,64,32]{3,1,2,0:T(4,128)(2,1)S(1)} %collective-permute-done.3), channel_id=1, source_target_pairs={{0,15},{1,0},{2,1},{3,2},{4,3},{5,4},{6,5},{7,6},{8,7},{9,8},{10,9... | collective-permute-start | bytes 49160 | tf_op jit(solution)/shard_map/ppermute | solution.py:55
  40.1 0.3 convolution_add_fusion.11
  40.4 1.6 collective-permute-done.4
  42.0 4.5 %collective-permute-start.5 = (bf16[1,4,64,32]{3,1,2,0:T(4,128)(2,1)S(1)}, bf16[1,4,64,32]{3,1,2,0:T(4,128)(2,1)S(1)}, u32[]{:S(2)}, u32[]{:S(2)}) collective-permute-start(bf16[1,4,64,32]{3,1,2,0:T(4,128)(2,1)S(1)} %collective-permute-done.4), channel_id=1, source_target_pairs={{0,15},{1,0},{2,1},{3,2},{4,3},{5,4},{6,5},{7,6},{8,7},{9,8},{10,9... | collective-permute-start | bytes 49160 | tf_op jit(solution)/shard_map/ppermute | solution.py:55
  46.5 0.3 convolution_add_fusion.10
  46.8 1.6 collective-permute-done.5
  48.4 4.5 %collective-permute-start.6 = (bf16[1,4,64,32]{3,1,2,0:T(4,128)(2,1)S(1)}, bf16[1,4,64,32]{3,1,2,0:T(4,128)(2,1)S(1)}, u32[]{:S(2)}, u32[]{:S(2)}) collective-permute-start(bf16[1,4,64,32]{3,1,2,0:T(4,128)(2,1)S(1)} %collective-permute-done.5), channel_id=1, source_target_pairs={{0,15},{1,0},{2,1},{3,2},{4,3},{5,4},{6,5},{7,6},{8,7},{9,8},{10,9... | collective-permute-start | bytes 49160 | tf_op jit(solution)/shard_map/ppermute | solution.py:55
  52.8 0.3 convolution_add_fusion.9
  53.2 1.6 collective-permute-done.6
  54.7 4.5 %collective-permute-start.7 = (bf16[1,4,64,32]{3,1,2,0:T(4,128)(2,1)S(1)}, bf16[1,4,64,32]{3,1,2,0:T(4,128)(2,1)S(1)}, u32[]{:S(2)}, u32[]{:S(2)}) collective-permute-start(bf16[1,4,64,32]{3,1,2,0:T(4,128)(2,1)S(1)} %collective-permute-done.6), channel_id=1, source_target_pairs={{0,15},{1,0},{2,1},{3,2},{4,3},{5,4},{6,5},{7,6},{8,7},{9,8},{10,9... | collective-permute-start | bytes 49160 | tf_op jit(solution)/shard_map/ppermute | solution.py:55
  59.2 0.3 convolution_add_fusion.8
  59.5 1.6 collective-permute-done.7
  61.1 4.5 %collective-permute-start.8 = (bf16[1,4,64,32]{3,1,2,0:T(4,128)(2,1)S(1)}, bf16[1,4,64,32]{3,1,2,0:T(4,128)(2,1)S(1)}, u32[]{:S(2)}, u32[]{:S(2)}) collective-permute-start(bf16[1,4,64,32]{3,1,2,0:T(4,128)(2,1)S(1)} %collective-permute-done.7), channel_id=1, source_target_pairs={{0,15},{1,0},{2,1},{3,2},{4,3},{5,4},{6,5},{7,6},{8,7},{9,8},{10,9... | collective-permute-start | bytes 49160 | tf_op jit(solution)/shard_map/ppermute | solution.py:55
  65.6 0.3 convolution_add_fusion.7
  65.9 1.6 collective-permute-done.8
  67.5 4.5 %collective-permute-start.9 = (bf16[1,4,64,32]{3,1,2,0:T(4,128)(2,1)S(1)}, bf16[1,4,64,32]{3,1,2,0:T(4,128)(2,1)S(1)}, u32[]{:S(2)}, u32[]{:S(2)}) collective-permute-start(bf16[1,4,64,32]{3,1,2,0:T(4,128)(2,1)S(1)} %collective-permute-done.8), channel_id=1, source_target_pairs={{0,15},{1,0},{2,1},{3,2},{4,3},{5,4},{6,5},{7,6},{8,7},{9,8},{10,9... | collective-permute-start | bytes 49160 | tf_op jit(solution)/shard_map/ppermute | solution.py:55
  72.0 0.3 convolution_add_fusion.6
  72.3 1.6 collective-permute-done.9
  73.9 4.5 %collective-permute-start.10 = (bf16[1,4,64,32]{3,1,2,0:T(4,128)(2,1)S(1)}, bf16[1,4,64,32]{3,1,2,0:T(4,128)(2,1)S(1)}, u32[]{:S(2)}, u32[]{:S(2)}) collective-permute-start(bf16[1,4,64,32]{3,1,2,0:T(4,128)(2,1)S(1)} %collective-permute-done.9), channel_id=1, source_target_pairs={{0,15},{1,0},{2,1},{3,2},{4,3},{5,4},{6,5},{7,6},{8,7},{9,8},{10,9... | collective-permute-start | bytes 49160 | tf_op jit(solution)/shard_map/ppermute | solution.py:55
  78.4 0.3 convolution_add_fusion.5
  78.7 1.6 collective-permute-done.10
  80.3 4.5 %collective-permute-start.11 = (bf16[1,4,64,32]{3,1,2,0:T(4,128)(2,1)S(1)}, bf16[1,4,64,32]{3,1,2,0:T(4,128)(2,1)S(1)}, u32[]{:S(2)}, u32[]{:S(2)}) collective-permute-start(bf16[1,4,64,32]{3,1,2,0:T(4,128)(2,1)S(1)} %collective-permute-done.10), channel_id=1, source_target_pairs={{0,15},{1,0},{2,1},{3,2},{4,3},{5,4},{6,5},{7,6},{8,7},{9,8},{10,9... | collective-permute-start | bytes 49160 | tf_op jit(solution)/shard_map/ppermute | solution.py:55
  84.8 0.3 convolution_add_fusion.4
  85.1 1.6 collective-permute-done.11
  86.7 4.5 %collective-permute-start.12 = (bf16[1,4,64,32]{3,1,2,0:T(4,128)(2,1)S(1)}, bf16[1,4,64,32]{3,1,2,0:T(4,128)(2,1)S(1)}, u32[]{:S(2)}, u32[]{:S(2)}) collective-permute-start(bf16[1,4,64,32]{3,1,2,0:T(4,128)(2,1)S(1)} %collective-permute-done.11), channel_id=1, source_target_pairs={{0,15},{1,0},{2,1},{3,2},{4,3},{5,4},{6,5},{7,6},{8,7},{9,8},{10,9... | collective-permute-start | bytes 49160 | tf_op jit(solution)/shard_map/ppermute | solution.py:55
  91.2 0.3 convolution_add_fusion.3
  91.5 1.6 collective-permute-done.12
  93.1 4.5 %collective-permute-start.13 = (bf16[1,4,64,32]{3,1,2,0:T(4,128)(2,1)S(1)}, bf16[1,4,64,32]{3,1,2,0:T(4,128)(2,1)S(1)}, u32[]{:S(2)}, u32[]{:S(2)}) collective-permute-start(bf16[1,4,64,32]{3,1,2,0:T(4,128)(2,1)S(1)} %collective-permute-done.12), channel_id=1, source_target_pairs={{0,15},{1,0},{2,1},{3,2},{4,3},{5,4},{6,5},{7,6},{8,7},{9,8},{10,9... | collective-permute-start | bytes 49160 | tf_op jit(solution)/shard_map/ppermute | solution.py:55
  97.6 0.3 convolution_add_fusion.2
  97.9 1.6 collective-permute-done.13
  99.5 4.5 %collective-permute-start.14 = (bf16[1,4,64,32]{3,1,2,0:T(4,128)(2,1)S(1)}, bf16[1,4,64,32]{3,1,2,0:T(4,128)(2,1)S(1)}, u32[]{:S(2)}, u32[]{:S(2)}) collective-permute-start(bf16[1,4,64,32]{3,1,2,0:T(4,128)(2,1)S(1)} %collective-permute-done.13), channel_id=1, source_target_pairs={{0,15},{1,0},{2,1},{3,2},{4,3},{5,4},{6,5},{7,6},{8,7},{9,8},{10,9... | collective-permute-start | bytes 49160 | tf_op jit(solution)/shard_map/ppermute | solution.py:55
  104.0 0.3 convolution_add_fusion.1
  104.3 1.6 collective-permute-done.14
  105.9 0.4 select_reduce_fusion
  106.3 34.0 %pmax.7 = f32[1,4,64]{2,1,0:T(4,128)S(1)} all-reduce(f32[1,4,64]{2,1,0:T(4,128)S(1)} %bitcast.161), channel_id=1, replica_groups=mesh['heads'=2,'seq'=16] {'seq'}, use_global_device_ids=true, to_apply=%region_3.4 | all-reduce | flops 256 | bytes 2048 | tf_op jit(solution)/shard_map/pmax | solution.py:79
  140.2 0.2 fusion.6
  140.5 0.4 fusion.2
  140.9 1.4 copy.157
  142.3 0.6 dynamic-slice
  143.5 0.1 copy.122
  144.3 29.8 %psum.14 = f32[4,64]{1,0:T(4,128)S(1)} all-reduce(f32[4,64]{1,0:T(4,128)S(1)} %get-tuple-element.8), channel_id=1, replica_groups=mesh['heads'=2,'seq'=16] {'seq'}, use_global_device_ids=true, to_apply=%region_6.7 | all-reduce | flops 256 | bytes 2048 | tf_op jit(solution)/shard_map/psum | solution.py:81
  174.0 59.6 %all-reduce.5.cloned.1.call-done = f32[1,4,64,512]{2,1,0,3:T(4,128)} async-done(((f32[1,4,64,512]{2,1,0,3:T(4,128)}), f32[1,4,64,512]{2,1,0,3:T(4,128)}) %all-reduce.5.cloned.1.call-update) | async-done | bytes 524304
  233.7 0.9 fusion.66
  234.5 0.1 copy.158
  234.7 0.4 convolution_bitcast_fusion
  235.1 59.3 %all-reduce.6 = bf16[32768]{0:T(1024)(128)(2,1)S(1)} all-reduce(f32[32768]{0:T(1024)S(1)} %bitcast.143), channel_id=3, replica_groups=mesh['heads'=2,'seq'=16] {'seq'}, use_global_device_ids=true, to_apply=%region_7.8.clone | all-reduce | flops 32768 | bytes 196608
  294.4 17.3 %all_gather.3 = bf16[32768]{0:T(1024)(128)(2,1)S(1)} all-gather(bf16[2048]{0:T(1024)(128)(2,1)S(1)} %dynamic-slice.10), channel_id=1, replica_groups=mesh['heads'=2,'seq'=16] {'seq'}, dimensions={0}, use_global_device_ids=true | all-gather | bytes 69632 | tf_op jit(solution)/shard_map/all_gather | solution.py:95
  311.7 5.1 %fusion.87 = f32[4,448]{1,0:T(4,128)S(1)} fusion(bf16[4,8192]{1,0:T(4,128)(2,1)S(1)} %reshape_reshape.3, bf16[8192,448]{0,1:T(8,128)(2,1)} %param.19), kind=kOutput, calls=%fused_computation.123 | convolution fusion | flops 29360128 | bytes 7412736 | tf_op jit(solution)/shard_map/dot_general | solution.py:97
  316.8 5.6 %psum.15 = bf16[4,448]{1,0:T(4,128)(2,1)} all-reduce(f32[4,448]{1,0:T(4,128)S(1)} %fusion.87), channel_id=1, replica_groups=mesh['heads'=2,'seq'=16] {'heads'}, use_global_device_ids=true, to_apply=%region_8.9 | all-reduce | flops 1792 | bytes 10752 | tf_op jit(solution)/shard_map/psum | solution.py:102
  (18 shorter events, 0.2 us)
Async XLA Ops:
  6.5 9.7 %copy-start = (bf16[1,512,512]{2,1,0:T(8,128)(2,1)S(1)}, bf16[1,512,512]{2,1,0:T(8,128)(2,1)}, u32[]{:S(2)}) copy-start(bf16[1,512,512]{2,1,0:T(8,128)(2,1)} %param.12) | copy-start | bytes 1572868
  6.5 227.1 %all-reduce.5.cloned.1.call-start = ((), (), s32[]{:S(2)}) async-start(), calls=%async_computation | async-start | bytes 2097152
  9.0 7.8 %collective-permute-start = (bf16[1,4,64,32]{3,1,2,0:T(4,128)(2,1)S(1)}, bf16[1,4,64,32]{3,1,2,0:T(4,128)(2,1)S(1)}, u32[]{:S(2)}, u32[]{:S(2)}) collective-permute-start(bf16[1,4,64,32]{3,1,2,0:T(4,128)(2,1)S(1)} %bitcast.145), channel_id=1, source_target_pairs={{0,15},{1,0},{2,1},{3,2},{4,3},{5,4},{6,5},{7,6},{8,7},{9,8},{10,9... | collective-permute-start | bytes 49160 | tf_op jit(solution)/shard_map/ppermute | solution.py:55
  16.8 6.0 %collective-permute-start.1 = (bf16[1,4,64,32]{3,1,2,0:T(4,128)(2,1)S(1)}, bf16[1,4,64,32]{3,1,2,0:T(4,128)(2,1)S(1)}, u32[]{:S(2)}, u32[]{:S(2)}) collective-permute-start(bf16[1,4,64,32]{3,1,2,0:T(4,128)(2,1)S(1)} %collective-permute-done), channel_id=1, source_target_pairs={{0,15},{1,0},{2,1},{3,2},{4,3},{5,4},{6,5},{7,6},{8,7},{9,8},{10,9... | collective-permute-start | bytes 49160 | tf_op jit(solution)/shard_map/ppermute | solution.py:55
  22.8 6.4 %collective-permute-start.2 = (bf16[1,4,64,32]{3,1,2,0:T(4,128)(2,1)S(1)}, bf16[1,4,64,32]{3,1,2,0:T(4,128)(2,1)S(1)}, u32[]{:S(2)}, u32[]{:S(2)}) collective-permute-start(bf16[1,4,64,32]{3,1,2,0:T(4,128)(2,1)S(1)} %collective-permute-done.1), channel_id=1, source_target_pairs={{0,15},{1,0},{2,1},{3,2},{4,3},{5,4},{6,5},{7,6},{8,7},{9,8},{10,9... | collective-permute-start | bytes 49160 | tf_op jit(solution)/shard_map/ppermute | solution.py:55
  29.2 6.4 %collective-permute-start.3 = (bf16[1,4,64,32]{3,1,2,0:T(4,128)(2,1)S(1)}, bf16[1,4,64,32]{3,1,2,0:T(4,128)(2,1)S(1)}, u32[]{:S(2)}, u32[]{:S(2)}) collective-permute-start(bf16[1,4,64,32]{3,1,2,0:T(4,128)(2,1)S(1)} %collective-permute-done.2), channel_id=1, source_target_pairs={{0,15},{1,0},{2,1},{3,2},{4,3},{5,4},{6,5},{7,6},{8,7},{9,8},{10,9... | collective-permute-start | bytes 49160 | tf_op jit(solution)/shard_map/ppermute | solution.py:55
  35.6 6.4 %collective-permute-start.4 = (bf16[1,4,64,32]{3,1,2,0:T(4,128)(2,1)S(1)}, bf16[1,4,64,32]{3,1,2,0:T(4,128)(2,1)S(1)}, u32[]{:S(2)}, u32[]{:S(2)}) collective-permute-start(bf16[1,4,64,32]{3,1,2,0:T(4,128)(2,1)S(1)} %collective-permute-done.3), channel_id=1, source_target_pairs={{0,15},{1,0},{2,1},{3,2},{4,3},{5,4},{6,5},{7,6},{8,7},{9,8},{10,9... | collective-permute-start | bytes 49160 | tf_op jit(solution)/shard_map/ppermute | solution.py:55
  42.0 6.4 %collective-permute-start.5 = (bf16[1,4,64,32]{3,1,2,0:T(4,128)(2,1)S(1)}, bf16[1,4,64,32]{3,1,2,0:T(4,128)(2,1)S(1)}, u32[]{:S(2)}, u32[]{:S(2)}) collective-permute-start(bf16[1,4,64,32]{3,1,2,0:T(4,128)(2,1)S(1)} %collective-permute-done.4), channel_id=1, source_target_pairs={{0,15},{1,0},{2,1},{3,2},{4,3},{5,4},{6,5},{7,6},{8,7},{9,8},{10,9... | collective-permute-start | bytes 49160 | tf_op jit(solution)/shard_map/ppermute | solution.py:55
  48.4 6.4 %collective-permute-start.6 = (bf16[1,4,64,32]{3,1,2,0:T(4,128)(2,1)S(1)}, bf16[1,4,64,32]{3,1,2,0:T(4,128)(2,1)S(1)}, u32[]{:S(2)}, u32[]{:S(2)}) collective-permute-start(bf16[1,4,64,32]{3,1,2,0:T(4,128)(2,1)S(1)} %collective-permute-done.5), channel_id=1, source_target_pairs={{0,15},{1,0},{2,1},{3,2},{4,3},{5,4},{6,5},{7,6},{8,7},{9,8},{10,9... | collective-permute-start | bytes 49160 | tf_op jit(solution)/shard_map/ppermute | solution.py:55
  54.7 6.4 %collective-permute-start.7 = (bf16[1,4,64,32]{3,1,2,0:T(4,128)(2,1)S(1)}, bf16[1,4,64,32]{3,1,2,0:T(4,128)(2,1)S(1)}, u32[]{:S(2)}, u32[]{:S(2)}) collective-permute-start(bf16[1,4,64,32]{3,1,2,0:T(4,128)(2,1)S(1)} %collective-permute-done.6), channel_id=1, source_target_pairs={{0,15},{1,0},{2,1},{3,2},{4,3},{5,4},{6,5},{7,6},{8,7},{9,8},{10,9... | collective-permute-start | bytes 49160 | tf_op jit(solution)/shard_map/ppermute | solution.py:55
  61.1 6.4 %collective-permute-start.8 = (bf16[1,4,64,32]{3,1,2,0:T(4,128)(2,1)S(1)}, bf16[1,4,64,32]{3,1,2,0:T(4,128)(2,1)S(1)}, u32[]{:S(2)}, u32[]{:S(2)}) collective-permute-start(bf16[1,4,64,32]{3,1,2,0:T(4,128)(2,1)S(1)} %collective-permute-done.7), channel_id=1, source_target_pairs={{0,15},{1,0},{2,1},{3,2},{4,3},{5,4},{6,5},{7,6},{8,7},{9,8},{10,9... | collective-permute-start | bytes 49160 | tf_op jit(solution)/shard_map/ppermute | solution.py:55
  65.6 76.6 %copy-start.2 = (u32[32]{0:T(128)S(1)}, u32[32]{0:T(128)}, u32[]{:S(2)}) copy-start(u32[32]{0:T(128)} %constant.132) | copy-start | bytes 388
  65.9 168.7 %copy-start.1 = (bf16[64,32,128]{2,1,0:T(8,128)(2,1)S(1)}, bf16[64,32,128]{2,1,0:T(8,128)(2,1)}, u32[]{:S(2)}) copy-start(bf16[64,32,128]{2,1,0:T(8,128)(2,1)} %param.17) | copy-start | bytes 1572868
  67.5 6.4 %collective-permute-start.9 = (bf16[1,4,64,32]{3,1,2,0:T(4,128)(2,1)S(1)}, bf16[1,4,64,32]{3,1,2,0:T(4,128)(2,1)S(1)}, u32[]{:S(2)}, u32[]{:S(2)}) collective-permute-start(bf16[1,4,64,32]{3,1,2,0:T(4,128)(2,1)S(1)} %collective-permute-done.8), channel_id=1, source_target_pairs={{0,15},{1,0},{2,1},{3,2},{4,3},{5,4},{6,5},{7,6},{8,7},{9,8},{10,9... | collective-permute-start | bytes 49160 | tf_op jit(solution)/shard_map/ppermute | solution.py:55
  73.9 6.4 %collective-permute-start.10 = (bf16[1,4,64,32]{3,1,2,0:T(4,128)(2,1)S(1)}, bf16[1,4,64,32]{3,1,2,0:T(4,128)(2,1)S(1)}, u32[]{:S(2)}, u32[]{:S(2)}) collective-permute-start(bf16[1,4,64,32]{3,1,2,0:T(4,128)(2,1)S(1)} %collective-permute-done.9), channel_id=1, source_target_pairs={{0,15},{1,0},{2,1},{3,2},{4,3},{5,4},{6,5},{7,6},{8,7},{9,8},{10,9... | collective-permute-start | bytes 49160 | tf_op jit(solution)/shard_map/ppermute | solution.py:55
  80.3 6.4 %collective-permute-start.11 = (bf16[1,4,64,32]{3,1,2,0:T(4,128)(2,1)S(1)}, bf16[1,4,64,32]{3,1,2,0:T(4,128)(2,1)S(1)}, u32[]{:S(2)}, u32[]{:S(2)}) collective-permute-start(bf16[1,4,64,32]{3,1,2,0:T(4,128)(2,1)S(1)} %collective-permute-done.10), channel_id=1, source_target_pairs={{0,15},{1,0},{2,1},{3,2},{4,3},{5,4},{6,5},{7,6},{8,7},{9,8},{10,9... | collective-permute-start | bytes 49160 | tf_op jit(solution)/shard_map/ppermute | solution.py:55
  86.7 6.4 %collective-permute-start.12 = (bf16[1,4,64,32]{3,1,2,0:T(4,128)(2,1)S(1)}, bf16[1,4,64,32]{3,1,2,0:T(4,128)(2,1)S(1)}, u32[]{:S(2)}, u32[]{:S(2)}) collective-permute-start(bf16[1,4,64,32]{3,1,2,0:T(4,128)(2,1)S(1)} %collective-permute-done.11), channel_id=1, source_target_pairs={{0,15},{1,0},{2,1},{3,2},{4,3},{5,4},{6,5},{7,6},{8,7},{9,8},{10,9... | collective-permute-start | bytes 49160 | tf_op jit(solution)/shard_map/ppermute | solution.py:55
  93.1 6.4 %collective-permute-start.13 = (bf16[1,4,64,32]{3,1,2,0:T(4,128)(2,1)S(1)}, bf16[1,4,64,32]{3,1,2,0:T(4,128)(2,1)S(1)}, u32[]{:S(2)}, u32[]{:S(2)}) collective-permute-start(bf16[1,4,64,32]{3,1,2,0:T(4,128)(2,1)S(1)} %collective-permute-done.12), channel_id=1, source_target_pairs={{0,15},{1,0},{2,1},{3,2},{4,3},{5,4},{6,5},{7,6},{8,7},{9,8},{10,9... | collective-permute-start | bytes 49160 | tf_op jit(solution)/shard_map/ppermute | solution.py:55
  99.5 6.4 %collective-permute-start.14 = (bf16[1,4,64,32]{3,1,2,0:T(4,128)(2,1)S(1)}, bf16[1,4,64,32]{3,1,2,0:T(4,128)(2,1)S(1)}, u32[]{:S(2)}, u32[]{:S(2)}) collective-permute-start(bf16[1,4,64,32]{3,1,2,0:T(4,128)(2,1)S(1)} %collective-permute-done.13), channel_id=1, source_target_pairs={{0,15},{1,0},{2,1},{3,2},{4,3},{5,4},{6,5},{7,6},{8,7},{9,8},{10,9... | collective-permute-start | bytes 49160 | tf_op jit(solution)/shard_map/ppermute | solution.py:55
Sparse Core Ops, SparseCore 0:
  142.4 91.2 all-reduce.4
